TPU v7x, 256 devices: a whole 4x4x8 slice. The times are simulated.
256 devices in a mesh: ta: 8 (over x, core), sa: 32 (over y, z).
Axes of the slice: x: 4, y: 4, z: 8, core: 2. Of those that a mesh axis runs over, the one named last changes fastest.
Arguments:
- scenes: bfloat16 [120, 4, 32, 256, 128], P('ta', None, 'sa'), may hold values from -48 to 48
- cloud_free: int32 [120, 32, 256, 128], P(None, None, ('ta', 'sa')), may hold values 0 or 1
Outputs:
- coefficients: float32 [8, 4, 32, 256, 128], P(None, None, None, ('ta', 'sa'))
- outlier_share: float32 [120, 4], replicated
All inputs are finite; a program needn't handle non-finite values. No bound on the sum of `cloud_free` on one device may be relied on, other than what follows from the above.
Results may differ from a plain program's by a relative error of at most 0.0003.
Values may be sent and summed in bfloat16 or wider, within the bound.
A program may use at most 128 MiB of HBM per device.

v0:
```python
import math

import jax
import jax.numpy as jnp
import numpy as np
from jax import lax
from jax.experimental import pallas as pl
from jax.experimental.pallas import tpu as pltpu
from jax.sharding import PartitionSpec as P

T = 120
HALF = 60
B = 4
K = 8
STRIPS = 32
LANES = 128
N_TA = 8
N_SA = 32
DATES = T // N_TA
TB = 24
MOMENTS = 21
RIDGE = 1.0
CAUCHY = 4.0
TINY = 1e-6
MESH = pl.DeviceIdType.MESH
F32 = jnp.float32
BF16 = jnp.bfloat16


def basis_table():
    p = (np.arange(T, dtype=np.float64) + 0.5) / T
    q = 2.0 * p - 1.0
    columns = [np.ones_like(p), q]
    for h in range(1, 7):
        columns += [np.cos(2.0 * math.pi * h * p), np.sin(2.0 * math.pi * h * p)]
    columns.append(q * q)
    for h in range(1, 4):
        columns += [q * np.cos(2.0 * math.pi * h * p), q * np.sin(2.0 * math.pi * h * p)]
    return np.stack(columns, axis=1)


def two_parts(table):
    high = table.astype(np.float32).astype(BF16)
    low = (table - high.astype(np.float64)).astype(np.float32).astype(BF16)
    return high, low


def tables():
    x = basis_table()
    eye = np.eye(8)
    high, low = two_parts(np.kron(x.T, eye))
    gram = np.concatenate([high, low], axis=0)
    dh, dl = two_parts(np.kron(x[:, :K], eye))
    fit = np.concatenate([dh, dh, dl], axis=1)
    return gram, fit


def gram_entry(m, i, j):
    if j == 0:
        return m[i]
    if j == 1:
        return m[14] if i == 1 else m[13 + i]
    a, b = i // 2, j // 2

    def sine(k):
        if k == 0:
            return None
        return m[2 * k + 1] if k > 0 else -m[-2 * k + 1]

    if i % 2 == 0 and j % 2 == 0:
        return 0.5 * (m[2 * (a - b)] + m[2 * (a + b)])
    if i % 2 == 1 and j % 2 == 1:
        return 0.5 * (m[2 * (a - b)] - m[2 * (a + b)])
    cos_h, sin_h = (a, b) if i % 2 == 0 else (b, a)
    other = sine(sin_h - cos_h)
    return 0.5 * m[2 * (a + b) + 1] if other is None else 0.5 * (m[2 * (a + b) + 1] + other)


def factor(m):
    lower, plain, inverse = {}, {}, []
    for j in range(K):
        for i in range(j, K):
            e = gram_entry(m, i, j)
            if i == j:
                e = e + RIDGE
            for k in range(j):
                e = e - lower[i, k] * plain[j, k]
            plain[i, j] = e
        inverse.append(1.0 / plain[j, j])
        for i in range(j + 1, K):
            lower[i, j] = plain[i, j] * inverse[j]
    return lower, inverse


def solve(lower, inverse, rhs):
    y = []
    for i in range(K):
        e = rhs[i]
        for k in range(i):
            e = e - lower[i, k] * y[k]
        y.append(e)
    x = [None] * K
    for i in reversed(range(K)):
        e = y[i] * inverse[i]
        for k in range(i + 1, K):
            e = e - lower[k, i] * x[k]
        x[i] = e
    return x


def dot(a, b):
    return jnp.dot(a, b, preferred_element_type=F32)


def rows(x):
    n = x.shape[0]
    return jnp.concatenate(
        [x[:, :8].reshape(n * 8, LANES), x[:, 8:].reshape(n * 8, LANES)], axis=1
    )


def blocks(x):
    n = x.shape[0] // 8
    return x[:, :LANES].reshape(n, 8, LANES), x[:, LANES:].reshape(n, 8, LANES)


def halves(x):
    high = x.astype(BF16)
    return high, (x - high.astype(F32)).astype(BF16)


def stacked(c):
    high, low = halves(c)
    return jnp.concatenate([high, low, high], axis=0)


def lane_sums(x):
    ones = jnp.ones((8, LANES), F32)
    out = lax.dot_general(
        ones, x, (((1,), (1,)), ((), ())), precision=lax.Precision.HIGHEST,
        preferred_element_type=F32,
    )
    return out[0:1]


def kernel(
    scn, msk, gram_in, fit_in, coef, share,
    val, mraw, pk, mrecv, wf, rr, zh, zl, yh, yl, gram, fit, fac, mom, c1, dl, csend,
    sred, s8, pay, b1, b2, tal, b3, b4,
    bulk_s, bulk_r, local, msk_s, msk_r, s1, r1, s2, r2, s3, r3, s4, r4, cs, cr,
):
    ta = lax.axis_index("ta")
    sa = lax.axis_index("sa")

    def to_ta(k):
        return {"ta": lax.rem(ta + k, N_TA)}

    def to_sa(k):
        return {"sa": lax.rem(sa + k, N_SA)}

    mask_in = pltpu.make_async_copy(msk, mraw, local.at[0])
    mask_in.start()
    gram_copy = pltpu.make_async_copy(gram_in, gram, local.at[1])
    gram_copy.start()
    fit_copy = pltpu.make_async_copy(fit_in, fit, local.at[2])
    fit_copy.start()
    mine = pltpu.make_async_copy(
        scn.at[:, :, pl.ds(pl.multiple_of(ta * 32, 32), 32)],
        val.at[pl.ds(ta * DATES, DATES)],
        local.at[3],
    )
    mine.start()

    barrier = pltpu.get_barrier_semaphore()

    def greet(k, carry):
        pl.semaphore_signal(barrier, inc=1, device_id=to_sa(k), device_id_type=MESH)
        return carry

    for k in range(1, N_TA):
        pl.semaphore_signal(barrier, inc=1, device_id=to_ta(k), device_id_type=MESH)
    lax.fori_loop(1, N_SA, greet, 0)
    pl.semaphore_wait(barrier, N_TA - 1 + N_SA - 1)

    def send_bulk(i, carry):
        b, h = i // 2, lax.rem(i, 2)
        for k in range(1, N_TA):
            t = lax.rem(ta + k, N_TA)
            pltpu.make_async_remote_copy(
                src_ref=scn.at[:, b, pl.ds(pl.multiple_of(t * 32 + h * 16, 16), 16)],
                dst_ref=val.at[pl.ds(ta * DATES, DATES), b, pl.ds(pl.multiple_of(h * 16, 16), 16)],
                send_sem=bulk_s.at[i],
                recv_sem=bulk_r.at[i],
                device_id={"ta": t},
                device_id_type=MESH,
            ).start()
        return carry

    lax.fori_loop(0, 2 * B, send_bulk, 0)

    mask_in.wait()

    def pack(i, carry):
        t = i * 4
        pk[pl.ds(t, 4)] = mraw[pl.ds(t, 4)] + mraw[pl.ds(t + HALF, 4)] * 65536
        return carry

    lax.fori_loop(0, HALF // 4, pack, 0)

    def send_mask(k, carry):
        j = lax.rem(sa + k, N_SA)
        pltpu.make_async_remote_copy(
            src_ref=pk.at[:, pl.ds(j, 1)],
            dst_ref=mrecv.at[:, pl.ds(sa, 1)],
            send_sem=msk_s,
            recv_sem=msk_r,
            device_id={"sa": j},
            device_id_type=MESH,
        ).start()
        return carry

    lax.fori_loop(1, N_SA, send_mask, 0)
    mrecv[:, pl.ds(sa, 1)] = pk[:, pl.ds(sa, 1)]
    some_rows = mrecv.at[:, pl.ds(0, N_SA - 1)]
    pltpu.make_async_copy(some_rows, some_rows, msk_r).wait()

    def unpack(i, carry):
        t = i * 4
        both = mrecv[pl.ds(t, 4)]
        wf[pl.ds(t, 4)] = (both & 65535).astype(F32)
        wf[pl.ds(t + HALF, 4)] = (both >> 16).astype(F32)
        return carry

    lax.fori_loop(0, HALF // 4, unpack, 0)
    sred[:, pl.ds(T, 8)] = jnp.zeros((B, 8, LANES), F32)
    for q in range(T // TB):
        w = wf[pl.ds(q * TB, TB)]
        w = (w[:, :8] + w[:, 8:16]) + (w[:, 16:24] + w[:, 24:])
        sred[0, pl.ds(q * TB, TB)] = jnp.sum(w, axis=1)
    counts_here = lane_sums(sred[0])
    pay[...] = jnp.zeros((8, LANES), F32)
    pay[4:5] = counts_here

    gram_copy.wait()
    fit_copy.wait()
    mine.wait()

    for h in range(2):
        for q in range(T // TB):
            zh[pl.ds(q * TB * 8, TB * 8)] = rows(
                wf[pl.ds(q * TB, TB), pl.ds(16 * h, 16)]
            ).astype(BF16)
        m = dot(gram[...], zh[...])
        m = m[: 8 * MOMENTS] + m[8 * MOMENTS :]
        lower, inverse = factor([m[8 * i : 8 * i + 8] for i in range(MOMENTS)])
        at = 0
        for j in range(K):
            for i in range(j + 1, K):
                fac[h, at] = lower[i, j]
                at += 1
        for j in range(K):
            fac[h, at + j] = inverse[j]

    def stored_factor(h):
        lower, at = {}, 0
        for j in range(K):
            for i in range(j + 1, K):
                lower[i, j] = fac[h, at]
                at += 1
        return lower, [fac[h, at + j] for j in range(K)]

    some_dates = T - DATES

    def first_pass(b, carry):
        for h in range(2):
            part = val.at[pl.ds(0, some_dates), b, pl.ds(16 * h, 16)]
            pltpu.make_async_copy(part, part, bulk_r.at[2 * b + h]).wait()
            for q in range(T // TB):
                v = val[pl.ds(q * TB, TB), b, pl.ds(16 * h, 16)].astype(F32)
                w = wf[pl.ds(q * TB, TB), pl.ds(16 * h, 16)]
                zh[pl.ds(q * TB * 8, TB * 8)] = rows(v * w).astype(BF16)
            table = jnp.concatenate(
                [gram[0 : 8 * K], gram[8 * MOMENTS : 8 * MOMENTS + 8 * K]], axis=0
            )
            m = dot(table, zh[...])
            m = m[: 8 * K] + m[8 * K :]
            lower, inverse = stored_factor(h)
            c = solve(lower, inverse, [m[8 * i : 8 * i + 8] for i in range(K)])
            c = jnp.concatenate(c, axis=0)
            c1[h, b] = c
            cc = stacked(c)
            for q in range(T // TB):
                v = val[pl.ds(q * TB, TB), b, pl.ds(16 * h, 16)].astype(F32)
                f0, f1 = blocks(dot(fit[pl.ds(q * TB * 8, TB * 8)], cc))
                r0, r1_ = v[:, :8] - f0, v[:, 8:] - f1
                w = wf[pl.ds(q * TB, TB), pl.ds(16 * h, 16)]
                rr[b, pl.ds(q * TB, TB), pl.ds(16 * h, 8)] = r0
                rr[b, pl.ds(q * TB, TB), pl.ds(16 * h + 8, 8)] = r1_
                total = jnp.sum(w[:, :8] * (r0 * r0) + w[:, 8:] * (r1_ * r1_), axis=1)
                if h == 0:
                    sred[b, pl.ds(q * TB, TB)] = total
                else:
                    sred[b, pl.ds(q * TB, TB)] += total
        return carry

    lax.fori_loop(0, B, first_pass, 0)

    def summed(own, near, far, near_s, near_r, far_s, far_r):
        for k in range(1, N_TA):
            pltpu.make_async_remote_copy(
                src_ref=own, dst_ref=near.at[k - 1], send_sem=near_s, recv_sem=near_r,
                device_id=to_ta(k), device_id_type=MESH,
            ).start()
        pltpu.make_async_copy(near, near, near_r).wait()
        total = own[...]
        for k in range(N_TA - 1):
            total = total + near[k]
        far[N_SA - 1] = total

        def send(k, carry):
            pltpu.make_async_remote_copy(
                src_ref=far.at[N_SA - 1], dst_ref=far.at[k - 1], send_sem=far_s, recv_sem=far_r,
                device_id=to_sa(k), device_id_type=MESH,
            ).start()
            return carry

        lax.fori_loop(1, N_SA, send, 0)
        others = far.at[pl.ds(0, N_SA - 1)]
        pltpu.make_async_copy(others, others, far_r).wait()
        total = far[0]
        for k in range(1, N_SA):
            total = total + far[k]
        pltpu.make_async_copy(near, near, near_s).wait()
        pltpu.make_async_copy(others, others, far_s).wait()
        return total

    for b in range(B):
        pay[b : b + 1] = lane_sums(sred[b])
    total = summed(pay, b1, b2, s1, r1, s2, r2)
    seen = total[4:5] + 1.0
    for b in range(B):
        spread = CAUCHY * (total[b : b + 1] + TINY) / seen
        column = jnp.transpose(jnp.broadcast_to(spread, (LANES, LANES)))
        s8[b] = jnp.broadcast_to(column[:T].reshape(T, 1, LANES), (T, 8, LANES))

    def robust_moments(b, carry):
        for h in range(2):
            for q in range(T // TB):
                dates = pl.ds(q * TB, TB)
                s = s8[b, dates]
                parts = []
                for g in range(2):
                    at = pl.ds(16 * h + 8 * g, 8)
                    r = rr[b, dates, at]
                    robust = wf[dates, at] * s / (s + r * r)
                    parts.append((robust.reshape(TB * 8, LANES), (robust * r).reshape(TB * 8, LANES)))
                z = jnp.concatenate([parts[0][0], parts[1][0]], axis=1)
                y = jnp.concatenate([parts[0][1], parts[1][1]], axis=1)
                out = pl.ds(q * TB * 8, TB * 8)
                zh[out], zl[out] = halves(z)
                yh[out], yl[out] = halves(y)
            m = dot(gram[...], zh[...])
            m = m[: 8 * MOMENTS] + m[8 * MOMENTS :] + dot(gram[: 8 * MOMENTS], zl[...])
            mom[h, b, pl.ds(0, 8 * MOMENTS)] = m
            table = jnp.concatenate(
                [gram[0 : 8 * K], gram[8 * MOMENTS : 8 * MOMENTS + 8 * K]], axis=0
            )
            m = dot(table, yh[...])
            m = m[: 8 * K] + m[8 * K :] + dot(gram[: 8 * K], yl[...])
            mom[h, b, pl.ds(8 * MOMENTS, 8 * K)] = m - c1[h, b]
        return carry

    lax.fori_loop(0, B, robust_moments, 0)

    def second_solve(i, carry):
        h, p = i // 2, lax.rem(i, 2) * 2

        def pair(ref, at):
            return jnp.concatenate([ref[h, p, pl.ds(at, 8)], ref[h, p + 1, pl.ds(at, 8)]], axis=1)

        lower, inverse = factor([pair(mom, 8 * k) for k in range(MOMENTS)])
        d = solve(lower, inverse, [pair(mom, 8 * (MOMENTS + k)) for k in range(K)])
        for k in range(K):
            c = pair(c1, 8 * k) + d[k]
            for j in range(2):
                dl[h, p + j, pl.ds(8 * k, 8)] = d[k][:, 256 * j : 256 * j + 256]
                for g in range(2):
                    lane = 256 * j + 128 * g
                    csend[4 * k + p + j, pl.ds(pl.multiple_of(16 * h + 8 * g, 8), 8)] = c[
                        :, lane : lane + 128
                    ]
        return carry

    lax.fori_loop(0, 4, second_solve, 0)

    def send_coef(k, carry):
        j = lax.rem(sa + k, N_SA)
        pltpu.make_async_remote_copy(
            src_ref=csend.at[:, pl.ds(j, 1)],
            dst_ref=coef.at[:, pl.ds(sa, 1)],
            send_sem=cs,
            recv_sem=cr,
            device_id={"sa": j},
            device_id_type=MESH,
        ).start()
        return carry

    lax.fori_loop(1, N_SA, send_coef, 0)
    coef[:, pl.ds(sa, 1)] = csend[:, pl.ds(sa, 1)]

    def final_pass(b, carry):
        for h in range(2):
            cc = stacked(dl[h, b])
            for q in range(T // TB):
                dates = pl.ds(q * TB, TB)
                f = blocks(dot(fit[pl.ds(q * TB * 8, TB * 8)], cc))
                s = s8[b, dates]
                terms = []
                for g in range(2):
                    at = pl.ds(16 * h + 8 * g, 8)
                    e = rr[b, dates, at] - f[g]
                    e = e * e
                    terms.append(wf[dates, at] * e / (e + s))
                part = jnp.sum(terms[0] + terms[1], axis=1)
                if h == 0:
                    sred[b, dates] = part
                else:
                    sred[b, dates] += part
        return carry

    lax.fori_loop(0, B, final_pass, 0)
    tal[...] = jnp.zeros((8, LANES), F32)
    for b in range(B):
        tal[b : b + 1] = lane_sums(sred[b])
    share[...] = summed(tal, b3, b4, s3, r3, s4, r4) / seen

    some_coefs = coef.at[:, pl.ds(0, N_SA - 1)]
    pltpu.make_async_copy(some_coefs, some_coefs, cr).wait()
    pltpu.make_async_copy(some_coefs, some_coefs, cs).wait()
    pltpu.make_async_copy(some_rows, some_rows, msk_s).wait()

    def sent_bulk(i, carry):
        part = val.at[pl.ds(0, some_dates), i // 2, pl.ds(pl.multiple_of(lax.rem(i, 2) * 16, 16), 16)]
        pltpu.make_async_copy(part, part, bulk_s.at[i]).wait()
        return carry

    lax.fori_loop(0, 2 * B, sent_bulk, 0)


def on_device(scenes, cloud_free):
    gram, fit = tables()
    vmem = pltpu.VMEM
    dma = pltpu.SemaphoreType.DMA
    coef, share = pl.pallas_call(
        kernel,
        out_shape=(
            jax.ShapeDtypeStruct((K * B, STRIPS, LANES), F32),
            jax.ShapeDtypeStruct((8, LANES), F32),
        ),
        in_specs=[pl.BlockSpec(memory_space=pl.ANY)] * 4,
        out_specs=(pl.BlockSpec(memory_space=vmem), pl.BlockSpec(memory_space=vmem)),
        scratch_shapes=[
            vmem((T, B, 32, LANES), BF16),
            vmem((T, 32, LANES), jnp.int32),
            vmem((HALF, 32, LANES), jnp.int32),
            vmem((HALF, 32, LANES), jnp.int32),
            vmem((T, 32, LANES), F32),
            vmem((B, T, 32, LANES), F32),
            vmem((T * 8, 256), BF16),
            vmem((T * 8, 256), BF16),
            vmem((T * 8, 256), BF16),
            vmem((T * 8, 256), BF16),
            vmem(gram.shape, BF16),
            vmem(fit.shape, BF16),
            vmem((2, 36, 8, 256), F32),
            vmem((2, B, 8 * (MOMENTS + K), 256), F32),
            vmem((2, B, 8 * K, 256), F32),
            vmem((2, B, 8 * K, 256), F32),
            vmem((K * B, 32, LANES), F32),
            vmem((B, LANES, LANES), F32),
            vmem((B, T, 8, LANES), F32),
            vmem((8, LANES), F32),
            vmem((N_TA - 1, 8, LANES), F32),
            vmem((N_SA, 8, LANES), F32),
            vmem((8, LANES), F32),
            vmem((N_TA - 1, 8, LANES), F32),
            vmem((N_SA, 8, LANES), F32),
            dma((2 * B,)),
            dma((2 * B,)),
            dma((4,)),
        ]
        + [dma] * 12,
        compiler_params=pltpu.CompilerParams(
            collective_id=0, has_side_effects=True, vmem_limit_bytes=60 * 2**20
        ),
    )(
        scenes.reshape(DATES, B, 256, LANES),
        cloud_free.reshape(T, STRIPS, LANES),
        jnp.asarray(gram),
        jnp.asarray(fit),
    )
    return coef.reshape(K, B, STRIPS, 1, LANES), share[:B, :T].T


def solution(mesh):
    return jax.shard_map(
        on_device,
        mesh=mesh,
        in_specs=(P("ta", None, "sa", None, None), P(None, None, ("ta", "sa"), None)),
        out_specs=(P(None, None, None, ("ta", "sa"), None), P()),
        check_vma=False,
    )
```

profile of v0, /device:TPU:1, one launch (start us, length us, event | category | flops | bytes accessed | tf_op | source)
XLA Modules:
  0.0 94.3 jit_solution(10149897316721843263)
XLA Ops:
  0.6 90.5 %shard_map.59 = (f32[32,32,128]{2,1,0:T(8,128)}, f32[8,128]{1,0:T(8,128)}) custom-call(bf16[15,4,256,128]{3,2,1,0:T(8,128)(2,1)} %bitcast.7, s32[120,32,128]{2,1,0:T(8,128)} %bitcast.8, bf16[336,960]{1,0:T(8,128)(2,1)} %constant.4.clone.gram_in, bf16[960,192]{1,0:T(8,128)(2,1)} %constant.5.clone.fit_in), custom_call_target="tpu_custom_call" | custom-call | tf_op jit(solution)/shard_map/pallas_call | solution.py:454
  91.2 1.3 %slice_bitcast_fusion = f32[120,4]{0,1:T(4,128)} fusion(f32[8,128]{1,0:T(8,128)} %get-tuple-element.5), kind=kLoop, calls=%fused_computation | loop fusion | bytes 3840 | tf_op jit(solution)/shard_map/transpose | solution.py:502
  92.4 1.9 %copy.8 = f32[8,4,32,1,128]{4,3,2,1,0:T(1,128)} copy(f32[8,4,32,1,128]{4,3,2,1,0:T(1,128)} %bitcast.9) | data formatting | bytes 1048576
where the time goes:
time: 95.7 us; the launch traced here: 94.3 us
  Pallas kernels  90.5 us (95%)
  local copies, waits for them, and re-layouts  3.12 us (3%)
    pallas_call x1, Pallas kernels, on_device(): pl.pallas_call(kernel, out_shape=(jax.ShapeDtypeStruct((K * B, STRIPS, LA...  90.5 us

commit v1 on v0

v1 whole, which is shorter than its diff:
```python
import math

import jax
import jax.numpy as jnp
import numpy as np
from jax import lax
from jax.experimental import pallas as pl
from jax.experimental.pallas import tpu as pltpu
from jax.sharding import PartitionSpec as P

T = 120
HALF = 60
B = 4
K = 8
STRIPS = 32
LANES = 128
N_TA = 8
N_SA = 32
N_Y = 4
N_Z = 8
DATES = T // N_TA
TB = 24
MOMENTS = 21
GROUP = 3
GROUP_ROWS = (3, 1, 1, 2, 2)
COUNTS = 0
VMEM_LIMIT = 62 * 2**20
RIDGE = 1.0
CAUCHY = 4.0
TINY = 1e-6
MESH = pl.DeviceIdType.MESH
F32 = jnp.float32
BF16 = jnp.bfloat16


def basis_table():
    p = (np.arange(T, dtype=np.float64) + 0.5) / T
    q = 2.0 * p - 1.0
    columns = [np.ones_like(p), q]
    for h in range(1, 7):
        columns += [np.cos(2.0 * math.pi * h * p), np.sin(2.0 * math.pi * h * p)]
    columns.append(q * q)
    for h in range(1, 4):
        columns += [q * np.cos(2.0 * math.pi * h * p), q * np.sin(2.0 * math.pi * h * p)]
    return np.stack(columns, axis=1)


def two_parts(table):
    high = table.astype(np.float32).astype(BF16)
    low = (table - high.astype(np.float64)).astype(np.float32).astype(BF16)
    return high, low


def tables():
    x = basis_table()
    eye = np.eye(8)
    high, low = two_parts(np.kron(x.T, eye))
    gram = np.concatenate([high, low], axis=0)
    dh, dl = two_parts(np.kron(x[:, :K], eye))
    fit = np.concatenate([dh, dh, dl], axis=1)
    return gram, fit


def gram_entry(m, i, j):
    if j == 0:
        return m[i]
    if j == 1:
        return m[14] if i == 1 else m[13 + i]
    a, b = i // 2, j // 2

    def sine(k):
        if k == 0:
            return None
        return m[2 * k + 1] if k > 0 else -m[-2 * k + 1]

    if i % 2 == 0 and j % 2 == 0:
        return 0.5 * (m[2 * (a - b)] + m[2 * (a + b)])
    if i % 2 == 1 and j % 2 == 1:
        return 0.5 * (m[2 * (a - b)] - m[2 * (a + b)])
    cos_h, sin_h = (a, b) if i % 2 == 0 else (b, a)
    other = sine(sin_h - cos_h)
    return 0.5 * m[2 * (a + b) + 1] if other is None else 0.5 * (m[2 * (a + b) + 1] + other)


def factor(m):
    lower, plain, inverse = {}, {}, []
    for j in range(K):
        for i in range(j, K):
            e = gram_entry(m, i, j)
            if i == j:
                e = e + RIDGE
            for k in range(j):
                e = e - lower[i, k] * plain[j, k]
            plain[i, j] = e
        inverse.append(1.0 / plain[j, j])
        for i in range(j + 1, K):
            lower[i, j] = plain[i, j] * inverse[j]
    return lower, inverse


def solve(lower, inverse, rhs):
    y = []
    for i in range(K):
        e = rhs[i]
        for k in range(i):
            e = e - lower[i, k] * y[k]
        y.append(e)
    x = [None] * K
    for i in reversed(range(K)):
        e = y[i] * inverse[i]
        for k in range(i + 1, K):
            e = e - lower[k, i] * x[k]
        x[i] = e
    return x


def dot(a, b):
    return jnp.dot(a, b, preferred_element_type=F32)


def rows(x):
    n = x.shape[0]
    return jnp.concatenate(
        [x[:, :8].reshape(n * 8, LANES), x[:, 8:].reshape(n * 8, LANES)], axis=1
    )


def blocks(x):
    n = x.shape[0] // 8
    return x[:, :LANES].reshape(n, 8, LANES), x[:, LANES:].reshape(n, 8, LANES)


def halves(x):
    high = x.astype(BF16)
    return high, (x - high.astype(F32)).astype(BF16)


def stacked(c):
    high, low = halves(c)
    return jnp.concatenate([high, low, high], axis=0)


def lane_sums(x):
    ones = jnp.ones((8, LANES), F32)
    out = lax.dot_general(
        ones, x, (((1,), (1,)), ((), ())), precision=lax.Precision.HIGHEST,
        preferred_element_type=F32,
    )
    return out[0:1]


def kernel(
    scn, msk, gram_in, fit_in, coef, share,
    val, mraw, pk, mrecv, wf, rr, zh, zl, yh, yl, gram, fit, fac, mom, c1, dl, csend,
    sred, s8, near, far,
    bulk_s, bulk_r, local, msk_s, msk_r, near_s, near_r, far_s, far_r, cs, cr, own_c, here,
):
    ta = lax.axis_index("ta")
    sa = lax.axis_index("sa")

    def to_ta(k):
        return {"ta": lax.rem(ta + k, N_TA)}

    def to_sa(k):
        return {"sa": lax.rem(sa + k, N_SA)}

    mask_in = pltpu.make_async_copy(msk, mraw, local.at[0])
    mask_in.start()
    gram_copy = pltpu.make_async_copy(gram_in, gram, local.at[1])
    gram_copy.start()
    fit_copy = pltpu.make_async_copy(fit_in, fit, local.at[2])
    fit_copy.start()
    mine = pltpu.make_async_copy(
        scn.at[:, :, pl.ds(pl.multiple_of(ta * 32, 32), 32)],
        val.at[pl.ds(ta * DATES, DATES)],
        local.at[3],
    )
    mine.start()

    y, z = sa // N_Z, lax.rem(sa, N_Z)

    def beside(dy, dz):
        return {"sa": lax.rem(y + dy + N_Y, N_Y) * N_Z + lax.rem(z + dz + N_Z, N_Z)}

    barrier = pltpu.get_barrier_semaphore()
    for k in range(1, N_TA):
        pl.semaphore_signal(barrier, inc=1, device_id=to_ta(k), device_id_type=MESH)
    for dy, dz in ((0, 1), (0, -1), (1, 0), (-1, 0)):
        pl.semaphore_signal(barrier, inc=1, device_id=beside(dy, dz), device_id_type=MESH)
    pl.semaphore_wait(barrier, N_TA - 1 + 4)

    def send_bulk(b, start, size, at):
        for k in range(1, N_TA):
            t = lax.rem(ta + k, N_TA)
            pltpu.make_async_remote_copy(
                src_ref=scn.at[:, b, pl.ds(pl.multiple_of(t * 32 + start, 16), size)],
                dst_ref=val.at[pl.ds(ta * DATES, DATES), b, pl.ds(start, size)],
                send_sem=bulk_s.at[at],
                recv_sem=bulk_r.at[at],
                device_id={"ta": t},
                device_id_type=MESH,
            ).start()

    def send_band(b, carry):
        send_bulk(b, 0, 32, b)
        return carry

    lax.fori_loop(0, B - 1, send_band, 0)

    mask_in.wait()

    def pack(i, carry):
        t = i * 4
        pk[pl.ds(t, 4)] = mraw[pl.ds(t, 4)] + mraw[pl.ds(t + HALF, 4)] * 65536
        return carry

    lax.fori_loop(0, HALF // 4, pack, 0)

    for at, pair in enumerate((((0, 1), (0, -1)), ((0, 2), (0, -2)), ((1, 0), (-1, 0)), ((1, 0), (-1, 0)))):
        for dy, dz in pair:
            pl.semaphore_signal(here.at[at], inc=1, device_id=beside(dy, dz), device_id_type=MESH)
        pl.semaphore_wait(here.at[at], 2)

    def send_mask(k, carry):
        j = lax.rem(sa + k, N_SA)
        pltpu.make_async_remote_copy(
            src_ref=pk.at[:, pl.ds(j, 1)],
            dst_ref=mrecv.at[:, pl.ds(sa, 1)],
            send_sem=msk_s,
            recv_sem=msk_r,
            device_id={"sa": j},
            device_id_type=MESH,
        ).start()
        return carry

    lax.fori_loop(1, N_SA, send_mask, 0)
    mrecv[:, pl.ds(sa, 1)] = pk[:, pl.ds(sa, 1)]
    gram_copy.wait()
    fit_copy.wait()
    mine.wait()
    some_rows = mrecv.at[:, pl.ds(0, N_SA - 1)]
    pltpu.make_async_copy(some_rows, some_rows, msk_r).wait()

    def unpack(i, carry):
        t = i * 4
        both = mrecv[pl.ds(t, 4)]
        wf[pl.ds(t, 4)] = (both & 65535).astype(F32)
        wf[pl.ds(t + HALF, 4)] = (both >> 16).astype(F32)
        return carry

    lax.fori_loop(0, HALF // 4, unpack, 0)

    def near_send(g):
        group = pl.ds(GROUP * g, GROUP_ROWS[g])
        for k in range(1, N_TA):
            pltpu.make_async_remote_copy(
                src_ref=near.at[group, pl.ds(N_TA - 1, 1)], dst_ref=near.at[group, pl.ds(k - 1, 1)],
                send_sem=near_s.at[g], recv_sem=near_r.at[g],
                device_id=to_ta(k), device_id_type=MESH,
            ).start()

    def far_send(g):
        group = pl.ds(GROUP * g, GROUP_ROWS[g])
        others = near.at[group, pl.ds(0, N_TA - 1)]
        pltpu.make_async_copy(others, others, near_r.at[g]).wait()
        for r in range(GROUP_ROWS[g]):
            far[GROUP * g + r, pl.ds(N_SA - 1, 1)] = jnp.sum(near[GROUP * g + r], axis=0, keepdims=True)

        def send(k):
            pltpu.make_async_remote_copy(
                src_ref=far.at[group, pl.ds(N_SA - 1, 1)], dst_ref=far.at[group, pl.ds(k - 1, 1)],
                send_sem=far_s.at[g], recv_sem=far_r.at[g],
                device_id=to_sa(k), device_id_type=MESH,
            ).start()

        def send_three(k, carry):
            send(k)
            send(k + 10)
            send(k + 20)
            return carry

        lax.fori_loop(1, 11, send_three, 0)
        send(N_SA - 1)

    def far_wait(g):
        others = far.at[pl.ds(GROUP * g, GROUP_ROWS[g]), pl.ds(0, N_SA - 1)]
        pltpu.make_async_copy(others, others, far_r.at[g]).wait()

    def far_sum(row):
        return jnp.sum(far[row], axis=0, keepdims=True)

    sred[pl.ds(T, 8)] = jnp.zeros((8, LANES), F32)
    for q in range(T // TB):
        w = wf[pl.ds(q * TB, TB)]
        w = (w[:, :8] + w[:, 8:16]) + (w[:, 16:24] + w[:, 24:])
        sred[pl.ds(q * TB, TB)] = jnp.sum(w, axis=1)
    near[COUNTS, pl.ds(N_TA - 1, 1)] = lane_sums(sred[...])

    for h in range(2):
        for q in range(T // TB):
            zh[pl.ds(q * TB * 8, TB * 8)] = rows(
                wf[pl.ds(q * TB, TB), pl.ds(16 * h, 16)]
            ).astype(BF16)
        m = dot(gram[...], zh[...])
        m = m[: 8 * MOMENTS] + m[8 * MOMENTS :]
        lower, inverse = factor([m[8 * i : 8 * i + 8] for i in range(MOMENTS)])
        at = 0
        for j in range(K):
            for i in range(j + 1, K):
                fac[h, at] = lower[i, j]
                at += 1
        for j in range(K):
            fac[h, at + j] = inverse[j]

    def stored_factor(h):
        lower, at = {}, 0
        for j in range(K):
            for i in range(j + 1, K):
                lower[i, j] = fac[h, at]
                at += 1
        return lower, [fac[h, at + j] for j in range(K)]

    some_dates = T - DATES

    def wait_bulk(b, h, sem):
        if h == 0:
            @pl.when(b < B - 1)
            def _():
                part = val.at[pl.ds(0, some_dates), b]
                pltpu.make_async_copy(part, part, sem.at[b]).wait()

        @pl.when(b == B - 1)
        def _():
            part = val.at[pl.ds(0, some_dates), b, pl.ds(16 * h, 16)]
            pltpu.make_async_copy(part, part, sem.at[B - 1 + h]).wait()

    def squares_row(b):
        return jnp.where(b < 2, b + 1, GROUP * (b - 1))

    def tally_row(b):
        return GROUP * 3 + b + b // 2

    def first_pass(b):
        for h in range(2):
            wait_bulk(b, h, bulk_r)
            for q in range(T // TB):
                v = val[pl.ds(q * TB, TB), b, pl.ds(16 * h, 16)].astype(F32)
                w = wf[pl.ds(q * TB, TB), pl.ds(16 * h, 16)]
                zh[pl.ds(q * TB * 8, TB * 8)] = rows(v * w).astype(BF16)
            table = jnp.concatenate(
                [gram[0 : 8 * K], gram[8 * MOMENTS : 8 * MOMENTS + 8 * K]], axis=0
            )
            m = dot(table, zh[...])
            m = m[: 8 * K] + m[8 * K :]
            lower, inverse = stored_factor(h)
            c = solve(lower, inverse, [m[8 * i : 8 * i + 8] for i in range(K)])
            c = jnp.concatenate(c, axis=0)
            c1[b, h] = c
            cc = stacked(c)
            for q in range(T // TB):
                v = val[pl.ds(q * TB, TB), b, pl.ds(16 * h, 16)].astype(F32)
                f0, f1 = blocks(dot(fit[pl.ds(q * TB * 8, TB * 8)], cc))
                r0, r1 = v[:, :8] - f0, v[:, 8:] - f1
                w = wf[pl.ds(q * TB, TB), pl.ds(16 * h, 16)]
                rr[b, pl.ds(q * TB, TB), pl.ds(16 * h, 8)] = r0
                rr[b, pl.ds(q * TB, TB), pl.ds(16 * h + 8, 8)] = r1
                total = jnp.sum(w[:, :8] * (r0 * r0) + w[:, 8:] * (r1 * r1), axis=1)
                if h == 0:
                    sred[pl.ds(q * TB, TB)] = total
                else:
                    sred[pl.ds(q * TB, TB)] += total
        near[squares_row(b), pl.ds(N_TA - 1, 1)] = lane_sums(sred[...])

    def send_coefs(b):
        def send(k, carry):
            j = lax.rem(sa + k, N_SA)
            pltpu.make_async_remote_copy(
                src_ref=csend.at[:, b, pl.ds(j, 1)],
                dst_ref=coef.at[:, b, pl.ds(sa, 1)],
                send_sem=cs.at[b],
                recv_sem=cr.at[b],
                device_id={"sa": j},
                device_id_type=MESH,
            ).start()
            return carry

        lax.fori_loop(1, N_SA, send, 0)
        pltpu.make_async_copy(
            csend.at[:, b, pl.ds(sa, 1)], coef.at[:, b, pl.ds(sa, 1)], own_c.at[b]
        ).start()

    def second_pass(b):
        spread = CAUCHY * (far_sum(squares_row(b)) + TINY) / (far_sum(COUNTS) + 1.0)
        column = jnp.transpose(jnp.broadcast_to(spread, (LANES, LANES)))
        s8[...] = jnp.broadcast_to(column[:T].reshape(T, 1, LANES), (T, 8, LANES))

        for h in range(2):
            for q in range(T // TB):
                dates = pl.ds(q * TB, TB)
                s = s8[dates]
                parts = []
                for g in range(2):
                    at = pl.ds(16 * h + 8 * g, 8)
                    r = rr[b, dates, at]
                    robust = wf[dates, at] * s / (s + r * r)
                    parts.append((robust.reshape(TB * 8, LANES), (robust * r).reshape(TB * 8, LANES)))
                z = jnp.concatenate([parts[0][0], parts[1][0]], axis=1)
                y = jnp.concatenate([parts[0][1], parts[1][1]], axis=1)
                out = pl.ds(q * TB * 8, TB * 8)
                zh[out], zl[out] = halves(z)
                yh[out], yl[out] = halves(y)
            m = dot(gram[...], zh[...])
            m = m[: 8 * MOMENTS] + m[8 * MOMENTS :] + dot(gram[: 8 * MOMENTS], zl[...])
            mom[h, pl.ds(0, 8 * MOMENTS)] = m
            table = jnp.concatenate(
                [gram[0 : 8 * K], gram[8 * MOMENTS : 8 * MOMENTS + 8 * K]], axis=0
            )
            m = dot(table, yh[...])
            m = m[: 8 * K] + m[8 * K :] + dot(gram[: 8 * K], yl[...])
            mom[h, pl.ds(8 * MOMENTS, 8 * K)] = m - c1[b, h]

        def both(at):
            return jnp.concatenate([mom[0, pl.ds(at, 8)], mom[1, pl.ds(at, 8)]], axis=1)

        lower, inverse = factor([both(8 * k) for k in range(MOMENTS)])
        d = solve(lower, inverse, [both(8 * (MOMENTS + k)) for k in range(K)])
        for k in range(K):
            for h in range(2):
                part = d[k][:, 256 * h : 256 * h + 256]
                dl[h, pl.ds(8 * k, 8)] = part
                c = c1[b, h, pl.ds(8 * k, 8)] + part
                csend[k, b, pl.ds(16 * h, 8)] = c[:, :LANES]
                csend[k, b, pl.ds(16 * h + 8, 8)] = c[:, LANES:]

        @pl.when(b == B - 1)
        def _():
            send_coefs(b)

        for h in range(2):
            cc = stacked(dl[h])
            for q in range(T // TB):
                dates = pl.ds(q * TB, TB)
                f = blocks(dot(fit[pl.ds(q * TB * 8, TB * 8)], cc))
                s = s8[dates]
                terms = []
                for g in range(2):
                    at = pl.ds(16 * h + 8 * g, 8)
                    e = rr[b, dates, at] - f[g]
                    e = e * e
                    terms.append(wf[dates, at] * e / (e + s))
                part = jnp.sum(terms[0] + terms[1], axis=1)
                if h == 0:
                    sred[dates] = part
                else:
                    sred[dates] += part
        near[tally_row(b), pl.ds(N_TA - 1, 1)] = lane_sums(sred[...])

    def step(i, carry):
        @pl.when((i < 2) | (i == 3) | (i == 6))
        def _():
            first_pass(jnp.where(i < 2, i, i // 3 + 1))

        @pl.when(i == 1)
        def _():
            near_send(0)
            send_bulk(B - 1, 0, 16, B - 1)

        @pl.when(i == 2)
        def _():
            far_send(0)

        @pl.when(i == 3)
        def _():
            near_send(1)
            send_bulk(B - 1, 16, 16, B)

        @pl.when(i == 4)
        def _():
            far_wait(0)

        @pl.when(i == 6)
        def _():
            near_send(2)

        @pl.when(i == 9)
        def _():
            far_wait(1)

        @pl.when(i == 10)
        def _():
            far_wait(2)

        @pl.when((i == 4) | (i == 7) | (i >= 9))
        def _():
            second_pass(jnp.where(i == 4, 0, jnp.where(i == 7, 1, i - 7)))

        @pl.when(i == 5)
        def _():
            far_send(1)
            send_coefs(0)

        @pl.when(i == 8)
        def _():
            near_send(3)
            far_send(2)
            send_coefs(1)

        @pl.when(i == 9)
        def _():
            send_coefs(2)
            far_send(3)

        return carry

    lax.fori_loop(0, 11, step, 0)
    near_send(4)
    far_send(4)
    far_wait(3)
    far_wait(4)
    for b in range(B):
        share[b : b + 1] = (far_sum(tally_row(b)) / (far_sum(COUNTS) + 1.0))[:, :T]

    def finish(b, carry):
        wait_bulk(b, 0, bulk_s)
        wait_bulk(b, 1, bulk_s)
        some_coefs = coef.at[:, b, pl.ds(0, N_SA - 1)]
        pltpu.make_async_copy(some_coefs, some_coefs, cr.at[b]).wait()
        pltpu.make_async_copy(some_coefs, some_coefs, cs.at[b]).wait()
        pltpu.make_async_copy(
            csend.at[:, b, pl.ds(sa, 1)], coef.at[:, b, pl.ds(sa, 1)], own_c.at[b]
        ).wait()
        return carry

    lax.fori_loop(0, B, finish, 0)
    pltpu.make_async_copy(some_rows, some_rows, msk_s).wait()

    for g, n in enumerate(GROUP_ROWS):
        rows_near = near.at[pl.ds(GROUP * g, n), pl.ds(0, N_TA - 1)]
        pltpu.make_async_copy(rows_near, rows_near, near_s.at[g]).wait()
        rows_far = far.at[pl.ds(GROUP * g, n), pl.ds(0, N_SA - 1)]
        pltpu.make_async_copy(rows_far, rows_far, far_s.at[g]).wait()


def handed_on(coef_in, share_in, coef_out, share_out, coef, share, sems):
    arrays = [(coef_in.at[k], coef.at[k], coef_out.at[k]) for k in range(K)]
    arrays.append((share_in, share, share_out))
    for i, (source, held, _) in enumerate(arrays):
        pltpu.make_async_copy(source, held, sems.at[0, i]).start()
    for i, (source, held, target) in enumerate(arrays):
        pltpu.make_async_copy(source, held, sems.at[0, i]).wait()
        pltpu.make_async_copy(held, target, sems.at[1, i]).start()
    for i, (_, held, target) in enumerate(arrays):
        pltpu.make_async_copy(held, target, sems.at[1, i]).wait()


def on_device(scenes, cloud_free):
    gram, fit = tables()
    vmem = pltpu.VMEM
    dma = pltpu.SemaphoreType.DMA
    results = (
        jax.ShapeDtypeStruct((K, B, STRIPS, LANES), F32),
        jax.ShapeDtypeStruct((B, T), F32),
    )
    anywhere = pl.BlockSpec(memory_space=pl.ANY)
    coef, share = pl.pallas_call(
        kernel,
        out_shape=results,
        in_specs=[anywhere] * 4,
        out_specs=(anywhere, pl.BlockSpec(memory_space=vmem)),
        scratch_shapes=[
            vmem((T, B, 32, LANES), BF16),
            vmem((T, 32, LANES), jnp.int32),
            vmem((HALF, 32, LANES), jnp.int32),
            vmem((HALF, 32, LANES), jnp.int32),
            vmem((T, 32, LANES), F32),
            vmem((B, T, 32, LANES), F32),
            vmem((T * 8, 256), BF16),
            vmem((T * 8, 256), BF16),
            vmem((T * 8, 256), BF16),
            vmem((T * 8, 256), BF16),
            vmem(gram.shape, BF16),
            vmem(fit.shape, BF16),
            vmem((2, 36, 8, 256), F32),
            vmem((2, 8 * (MOMENTS + K), 256), F32),
            vmem((B, 2, 8 * K, 256), F32),
            vmem((2, 8 * K, 256), F32),
            vmem((K, B, 32, LANES), F32),
            vmem((LANES, LANES), F32),
            vmem((T, 8, LANES), F32),
            vmem((GROUP * len(GROUP_ROWS), N_TA, LANES), F32),
            vmem((GROUP * len(GROUP_ROWS), N_SA, LANES), F32),
            dma((B + 1,)),
            dma((B + 1,)),
            dma((4,)),
            dma,
            dma,
            dma((len(GROUP_ROWS),)),
            dma((len(GROUP_ROWS),)),
            dma((len(GROUP_ROWS),)),
            dma((len(GROUP_ROWS),)),
            dma((B,)),
            dma((B,)),
            dma((B,)),
            pltpu.SemaphoreType.REGULAR((4,)),
        ],
        compiler_params=pltpu.CompilerParams(
            collective_id=0, has_side_effects=True, vmem_limit_bytes=VMEM_LIMIT
        ),
    )(
        scenes.reshape(DATES, B, 256, LANES),
        cloud_free.reshape(T, STRIPS, LANES),
        jnp.asarray(gram),
        jnp.asarray(fit),
    )
    coef, share = pl.pallas_call(
        handed_on,
        out_shape=results,
        in_specs=[anywhere] * 2,
        out_specs=(anywhere, anywhere),
        scratch_shapes=[
            vmem((K, B, STRIPS, LANES), F32),
            vmem((B, T), F32),
            dma((2, K + 1)),
        ],
    )(coef, share)
    return coef.reshape(K, B, STRIPS, 1, LANES), share.T


def solution(mesh):
    return jax.shard_map(
        on_device,
        mesh=mesh,
        in_specs=(P("ta", None, "sa", None, None), P(None, None, ("ta", "sa"), None)),
        out_specs=(P(None, None, None, ("ta", "sa"), None), P()),
        check_vma=False,
    )
```

time: 95.7 us -> 84.7 us (0.89); the launches traced: 94.3 us -> 84.6 us
  Pallas kernels: 90.5 us -> 84 us
  local copies, waits for them, and re-layouts: 3.12 us -> 0 us
    pallas_call x1 -> x2, Pallas kernels: 90.5 us -> 84 us  [the longest x1 82.1 us: on_device(): pl.pallas_call(kernel, out_shape=results, in_specs=[anywhere] * 4, out_sp...]
    unnamed x1 -> x0, local copies, waits for them, and re-layouts: 1.87 us -> none
    transpose x1 -> x0, local copies, waits for them, and re-layouts: 1.25 us -> none  [on_device(): return (coef.reshape(K, B, STRIPS, 1, LANES), share[:B, :T].T)]
where the time goes in v1:
time: 84.7 us; the launch traced here: 84.6 us
  Pallas kernels  84 us (99%)
    pallas_call x1, Pallas kernels, on_device(): pl.pallas_call(kernel, out_shape=results, in_specs=[anywhere] * 4, out_sp...  82.1 us
    pallas_call x1, Pallas kernels, on_device(): pl.pallas_call(handed_on, out_shape=results, in_specs=[anywhere] * 2, out...  1.85 us

profile of v1, /device:TPU:1, one launch (start us, length us, event | category | flops | bytes accessed | tf_op | source)
XLA Modules:
  0.0 84.6 jit_solution(18183657410382468777)
XLA Ops:
  0.6 82.1 %shard_map.59 = (f32[8,4,32,128]{3,2,1,0:T(8,128)}, f32[4,120]{1,0:T(4,128)}) custom-call(bf16[15,4,256,128]{3,2,1,0:T(8,128)(2,1)} %bitcast.6, s32[120,32,128]{2,1,0:T(8,128)} %bitcast.7, bf16[336,960]{1,0:T(8,128)(2,1)} %constant.4.clone.gram_in, bf16[960,192]{1,0:T(8,128)(2,1)} %constant.5.clone.fit_in), custom_call_target="tpu_custom_call" | custom-call | tf_op jit(solution)/shard_map/pallas_call | solution.py:565
  82.8 1.9 %shard_map.60 = (f32[8,4,32,128]{3,2,1,0:T(8,128)}, f32[4,120]{1,0:T(4,128)}) custom-call(f32[8,4,32,128]{3,2,1,0:T(8,128)} %get-tuple-element.6.coef_in, f32[4,120]{1,0:T(4,128)} %get-tuple-element.7.share_in), custom_call_target="tpu_custom_call" | custom-call | tf_op jit(solution)/shard_map/pallas_call | solution.py:615

commit v2 on v1

--- a/solution.py
+++ b/solution.py
@@ -206,6 +206,7 @@
         return carry
 
     lax.fori_loop(0, B - 1, send_band, 0)
+    send_bulk(B - 1, 0, 16, B - 1)
 
     mask_in.wait()
 
@@ -456,63 +457,63 @@
         near[tally_row(b), pl.ds(N_TA - 1, 1)] = lane_sums(sred[...])
 
     def step(i, carry):
-        @pl.when((i < 2) | (i == 3) | (i == 6))
-        def _():
-            first_pass(jnp.where(i < 2, i, i // 3 + 1))
+        @pl.when((i < 3) | (i == 4))
+        def _():
+            first_pass(jnp.where(i < 3, i, B - 1))
 
         @pl.when(i == 1)
         def _():
             near_send(0)
-            send_bulk(B - 1, 0, 16, B - 1)
+            send_bulk(B - 1, 16, 16, B)
 
         @pl.when(i == 2)
         def _():
+            near_send(1)
+
+        @pl.when(i == 3)
+        def _():
             far_send(0)
 
-        @pl.when(i == 3)
-        def _():
-            near_send(1)
-            send_bulk(B - 1, 16, 16, B)
-
         @pl.when(i == 4)
         def _():
+            near_send(2)
+            far_send(1)
+
+        @pl.when(i == 5)
+        def _():
             far_wait(0)
 
+        @pl.when(i == 7)
+        def _():
+            far_wait(1)
+
+        @pl.when(i == 8)
+        def _():
+            far_wait(2)
+
+        @pl.when(i >= 5)
+        def _():
+            second_pass(i - 5)
+
+        @pl.when(i == 5)
+        def _():
+            far_send(2)
+
+        @pl.when((i >= 5) & (i < 8))
+        def _():
+            send_coefs(i - 5)
+
         @pl.when(i == 6)
         def _():
-            near_send(2)
-
-        @pl.when(i == 9)
-        def _():
-            far_wait(1)
-
-        @pl.when(i == 10)
-        def _():
-            far_wait(2)
-
-        @pl.when((i == 4) | (i == 7) | (i >= 9))
-        def _():
-            second_pass(jnp.where(i == 4, 0, jnp.where(i == 7, 1, i - 7)))
-
-        @pl.when(i == 5)
-        def _():
-            far_send(1)
-            send_coefs(0)
-
-        @pl.when(i == 8)
-        def _():
             near_send(3)
-            far_send(2)
-            send_coefs(1)
-
-        @pl.when(i == 9)
-        def _():
-            send_coefs(2)
+
+        @pl.when(i == 7)
+        def _():
             far_send(3)
 
         return carry
 
-    lax.fori_loop(0, 11, step, 0)
+    lax.fori_loop(0, 9, step, 0)
     near_send(4)
     far_send(4)
     far_wait(3)

time: 84.7 us -> 82.6 us (0.975)
  Pallas kernels: 84 us -> 81.8 us
    pallas_call x1, Pallas kernels: 82.1 us -> 79.9 us  [on_device(): pl.pallas_call(kernel, out_shape=results, in_specs=[anywhere] * 4, out_sp...]
where the time goes in v2:
time: 82.6 us; the launch traced here: 82.4 us
  Pallas kernels  81.8 us (99%)
    pallas_call x1, Pallas kernels, on_device(): pl.pallas_call(kernel, out_shape=results, in_specs=[anywhere] * 4, out_sp...  79.9 us
    pallas_call x1, Pallas kernels, on_device(): pl.pallas_call(handed_on, out_shape=results, in_specs=[anywhere] * 2, out...  1.85 us

profile of v2, /device:TPU:1, one launch (start us, length us, event | category | flops | bytes accessed | tf_op | source)
XLA Modules:
  0.0 82.4 jit_solution(2599246905501730787)
XLA Ops:
  0.6 79.9 %shard_map.59 = (f32[8,4,32,128]{3,2,1,0:T(8,128)}, f32[4,120]{1,0:T(4,128)}) custom-call(bf16[15,4,256,128]{3,2,1,0:T(8,128)(2,1)} %bitcast.6, s32[120,32,128]{2,1,0:T(8,128)} %bitcast.7, bf16[336,960]{1,0:T(8,128)(2,1)} %constant.4.clone.gram_in, bf16[960,192]{1,0:T(8,128)(2,1)} %constant.5.clone.fit_in), custom_call_target="tpu_custom_call" | custom-call | tf_op jit(solution)/shard_map/pallas_call | solution.py:566
  80.6 1.9 %shard_map.60 = (f32[8,4,32,128]{3,2,1,0:T(8,128)}, f32[4,120]{1,0:T(4,128)}) custom-call(f32[8,4,32,128]{3,2,1,0:T(8,128)} %get-tuple-element.6.coef_in, f32[4,120]{1,0:T(4,128)} %get-tuple-element.7.share_in), custom_call_target="tpu_custom_call" | custom-call | tf_op jit(solution)/shard_map/pallas_call | solution.py:616

commit v3 on v2

--- a/solution.py
+++ b/solution.py
@@ -24,6 +24,7 @@
 GROUP = 3
 GROUP_ROWS = (3, 1, 1, 2, 2)
 COUNTS = 0
+FAR_FIRST = (4, 5, 3, 2, 6, 7, 1)
 VMEM_LIMIT = 62 * 2**20
 RIDGE = 1.0
 CAUCHY = 4.0
@@ -190,7 +191,7 @@
     pl.semaphore_wait(barrier, N_TA - 1 + 4)
 
     def send_bulk(b, start, size, at):
-        for k in range(1, N_TA):
+        for k in FAR_FIRST:
             t = lax.rem(ta + k, N_TA)
             pltpu.make_async_remote_copy(
                 src_ref=scn.at[:, b, pl.ds(pl.multiple_of(t * 32 + start, 16), size)],
@@ -274,13 +275,12 @@
                 device_id=to_sa(k), device_id_type=MESH,
             ).start()
 
-        def send_three(k, carry):
-            send(k)
-            send(k + 10)
-            send(k + 20)
+        def send_six(k, carry):
+            for more in range(0, 30, 5):
+                send(k + more)
             return carry
 
-        lax.fori_loop(1, 11, send_three, 0)
+        lax.fori_loop(1, 6, send_six, 0)
         send(N_SA - 1)
 
     def far_wait(g):
@@ -373,7 +373,7 @@
         near[squares_row(b), pl.ds(N_TA - 1, 1)] = lane_sums(sred[...])
 
     def send_coefs(b):
-        def send(k, carry):
+        def send(k):
             j = lax.rem(sa + k, N_SA)
             pltpu.make_async_remote_copy(
                 src_ref=csend.at[:, b, pl.ds(j, 1)],
@@ -383,9 +383,14 @@
                 device_id={"sa": j},
                 device_id_type=MESH,
             ).start()
+
+        def send_six(k, carry):
+            for more in range(0, 30, 5):
+                send(k + more)
             return carry
 
-        lax.fori_loop(1, N_SA, send, 0)
+        lax.fori_loop(1, 6, send_six, 0)
+        send(N_SA - 1)
         pltpu.make_async_copy(
             csend.at[:, b, pl.ds(sa, 1)], coef.at[:, b, pl.ds(sa, 1)], own_c.at[b]
         ).start()
@@ -507,14 +512,11 @@
         def _():
             near_send(3)
 
-        @pl.when(i == 7)
-        def _():
-            far_send(3)
-
         return carry
 
     lax.fori_loop(0, 9, step, 0)
     near_send(4)
+    far_send(3)
     far_send(4)
     far_wait(3)
     far_wait(4)

time: 82.6 us -> 81.4 us (0.985)
  Pallas kernels: 81.8 us -> 80.7 us
    pallas_call x1, Pallas kernels: 79.9 us -> 78.8 us  [on_device(): pl.pallas_call(kernel, out_shape=results, in_specs=[anywhere] * 4, out_sp...]
where the time goes in v3:
time: 81.4 us; the launch traced here: 81.3 us
  Pallas kernels  80.7 us (99%)
    pallas_call x1, Pallas kernels, on_device(): pl.pallas_call(kernel, out_shape=results, in_specs=[anywhere] * 4, out_sp...  78.8 us
    pallas_call x1, Pallas kernels, on_device(): pl.pallas_call(handed_on, out_shape=results, in_specs=[anywhere] * 2, out...  1.85 us

profile of v3, /device:TPU:1, one launch (start us, length us, event | category | flops | bytes accessed | tf_op | source)
XLA Modules:
  0.0 81.3 jit_solution(14559743005921254072)
XLA Ops:
  0.6 78.8 %shard_map.59 = (f32[8,4,32,128]{3,2,1,0:T(8,128)}, f32[4,120]{1,0:T(4,128)}) custom-call(bf16[15,4,256,128]{3,2,1,0:T(8,128)(2,1)} %bitcast.6, s32[120,32,128]{2,1,0:T(8,128)} %bitcast.7, bf16[336,960]{1,0:T(8,128)(2,1)} %constant.4.clone.gram_in, bf16[960,192]{1,0:T(8,128)(2,1)} %constant.5.clone.fit_in), custom_call_target="tpu_custom_call" | custom-call | tf_op jit(solution)/shard_map/pallas_call | solution.py:568
  79.4 1.9 %shard_map.60 = (f32[8,4,32,128]{3,2,1,0:T(8,128)}, f32[4,120]{1,0:T(4,128)}) custom-call(f32[8,4,32,128]{3,2,1,0:T(8,128)} %get-tuple-element.6.coef_in, f32[4,120]{1,0:T(4,128)} %get-tuple-element.7.share_in), custom_call_target="tpu_custom_call" | custom-call | tf_op jit(solution)/shard_map/pallas_call | solution.py:618
